TPU v7x, 8 devices: a whole 2x2x1 slice. The times are simulated.
8 devices in a mesh: stage: 1 (over z), data: 8 (over y, x, core).
Axes of the slice: x: 2, y: 2, z: 1, core: 2. Of those that a mesh axis runs over, the one named last changes fastest.
Arguments:
- grad_attn: float32 [8, 2, 2048, 2048], P(('stage', 'data'))
- mom_attn: float32 [2, 2048, 2048], P('stage', 'data')
- master_attn: float32 [2, 2048, 2048], P('stage', 'data')
- grad_up: float32 [8, 4, 2048, 1408], P(('stage', 'data'))
- mom_up: float32 [4, 2048, 1408], P('stage', 'data')
- master_up: float32 [4, 2048, 1408], P('stage', 'data')
- grad_down: float32 [8, 4, 1408, 2048], P(('stage', 'data'))
- mom_down: float32 [4, 1408, 2048], P('stage', 'data')
- master_down: float32 [4, 1408, 2048], P('stage', 'data')
Outputs:
- output 1: float32 [2, 2048, 2048], P('stage', 'data')
- output 2: float32 [2, 2048, 2048], P('stage', 'data')
- output 3: bfloat16 [2, 2048, 2048], P('stage', 'data')
- output 4: float32 [4, 2048, 1408], P('stage', 'data')
- output 5: float32 [4, 2048, 1408], P('stage', 'data')
- output 6: bfloat16 [4, 2048, 1408], P('stage', 'data')
- output 7: float32 [4, 1408, 2048], P('stage', 'data')
- output 8: float32 [4, 1408, 2048], P('stage', 'data')
- output 9: bfloat16 [4, 1408, 2048], P('stage', 'data')
All inputs are finite; a program needn't handle non-finite values.
Results may differ from a plain program's by a relative error of at most 0.00648393.
Values are sent between devices in bfloat16 or wider.
A program may use at most 1 GiB of HBM per device.

v0:
```python
import math
import functools
import jax
import jax.numpy as jnp
from jax import lax
from jax.sharding import PartitionSpec as P, NamedSharding

MOMENTUM = 0.95
LEARN_RATE = 0.25
WEIGHT_DECAY = 0.2
EPSILON = 1e-7
COEF_A = 3.4445
COEF_B = -4.7750
COEF_C = 2.0315
NS_STEPS = 5


def newton_schulz(x_mat, is_tall):
    for _ in range(NS_STEPS):
        if is_tall:
            gram_mat = jnp.einsum('bkr,bkc->brc', x_mat, x_mat, preferred_element_type=jnp.float32)
        else:
            gram_mat = jnp.einsum('brk,bck->brc', x_mat, x_mat, preferred_element_type=jnp.float32)
        gram_mat = gram_mat.astype(jnp.bfloat16)
        gram_sq = jnp.einsum('brk,bkc->brc', gram_mat, gram_mat, preferred_element_type=jnp.float32).astype(jnp.bfloat16)
        poly_mat = (COEF_B * gram_mat.astype(jnp.float32) + COEF_C * gram_sq.astype(jnp.float32)).astype(jnp.bfloat16)
        if is_tall:
            update = jnp.einsum('bkc,brc->bkr', x_mat, poly_mat, preferred_element_type=jnp.float32)
        else:
            update = jnp.einsum('brc,bck->brk', poly_mat, x_mat, preferred_element_type=jnp.float32)
        x_mat = (COEF_A * x_mat.astype(jnp.float32) + update.astype(jnp.bfloat16).astype(jnp.float32)).astype(jnp.bfloat16)
    return x_mat


def stack_step(grad_all, mom_old, master_old, offset, group_size):
    count, rows_local, n_cols = mom_old.shape
    n_rows = rows_local * group_size
    grad_rows = lax.psum_scatter(grad_all[0], 'data', scatter_dimension=1, tiled=True) / group_size
    mom_new = MOMENTUM * mom_old + grad_rows
    norm_sq = lax.psum(jnp.sum(mom_new * mom_new, axis=(1, 2)), 'data')
    x_rows = (mom_new / (jnp.sqrt(norm_sq)[:, None, None] + EPSILON)).astype(jnp.bfloat16)
    slots = (count + offset + group_size - 1) // group_size
    padded = jnp.pad(x_rows, ((offset, slots * group_size - count - offset), (0, 0), (0, 0)))
    send_buf = padded.reshape(slots, group_size, rows_local, n_cols)
    owned = lax.all_to_all(send_buf, 'data', 1, 2, tiled=True).reshape(slots, n_rows, n_cols)
    positions = jnp.arange(slots) * group_size + lax.axis_index('data')
    has_work = jnp.any((positions >= offset) & (positions < offset + count))
    ortho_mat = lax.cond(has_work, functools.partial(newton_schulz, is_tall=n_rows > n_cols), jnp.zeros_like, owned)
    returned = lax.all_to_all(ortho_mat.reshape(slots, 1, n_rows, n_cols), 'data', 2, 1, tiled=True)
    ortho_rows = returned.reshape(slots * group_size, rows_local, n_cols)[offset:offset + count]
    scale = 0.2 * math.sqrt(max(n_rows, n_cols))
    master_new = master_old - LEARN_RATE * (scale * ortho_rows.astype(jnp.float32) + WEIGHT_DECAY * master_old)
    return [mom_new, master_new, master_new.astype(jnp.bfloat16)]


def solution(mesh):
    group_size = mesh.shape['data']
    grad_spec = P(('stage', 'data'), None, None, None)
    row_spec = P('stage', 'data', None)

    def step_local(*arrays):
        attn_count = arrays[1].shape[0]
        expert_count = arrays[4].shape[0]
        offsets = (0, attn_count % group_size, (attn_count + expert_count) % group_size)
        results = []
        for stack_idx in range(3):
            results.extend(stack_step(arrays[3 * stack_idx], arrays[3 * stack_idx + 1], arrays[3 * stack_idx + 2], offsets[stack_idx], group_size))
        return tuple(results)

    in_specs = (grad_spec, row_spec, row_spec) * 3
    out_specs = (row_spec,) * 9
    return jax.shard_map(step_local, mesh=mesh, in_specs=in_specs, out_specs=out_specs, check_vma=False)
```

profile of v0, /device:TPU:0, one launch (start us, length us, event | category | flops | bytes accessed | tf_op | source)
XLA Modules:
  0.0 2229.0 jit_solution(1822295874318443742)
XLA Ops:
  9.4 201.2 %reduce-scatter.4.cloned.1.call-done = f32[2,256,2048]{2,1,0:T(8,128)} async-done(((f32[2,2048,2048]{2,1,0:T(8,128)}), f32[2,256,2048]{2,1,0:T(8,128)}) %reduce-scatter.4.cloned.1.call-update) | async-done | bytes 4194320 | tf_op jit(solution)/shard_map/reduce_scatter | solution.py:38
  217.2 252.1 %reduce-scatter.8.cloned.1.call-done = f32[4,176,2048]{2,1,0:T(8,128)} async-done(((f32[4,1408,2048]{2,1,0:T(8,128)}), f32[4,176,2048]{2,1,0:T(8,128)}) %reduce-scatter.8.cloned.1.call-update) | async-done | bytes 5767184 | tf_op jit(solution)/shard_map/reduce_scatter | solution.py:38
  477.6 250.4 %reduce-scatter.6.cloned.1.call-done = f32[4,256,1408]{2,1,0:T(8,128)} async-done(((f32[4,2048,1408]{2,1,0:T(8,128)}), f32[4,256,1408]{2,1,0:T(8,128)}) %reduce-scatter.6.cloned.1.call-update) | async-done | bytes 5767184 | tf_op jit(solution)/shard_map/reduce_scatter | solution.py:38
  774.7 58.8 %all-to-all-done.2 = bf16[1,8,256,1408]{3,2,0,1:T(8,128)(2,1)} async-done(((bf16[1,8,256,1408]{3,2,0,1:T(8,128)(2,1)}), bf16[1,8,256,1408]{3,2,0,1:T(8,128)(2,1)}, u32[]{:S(2)}, u32[]{:S(2)}) %all-to-all-start.2) | async-done | bytes 5767200 | tf_op jit(solution)/shard_map/all_to_all | solution.py:45
  856.1 75.1 %all-to-all-done = bf16[1,8,256,2048]{3,2,0,1:T(8,128)(2,1)} async-done(((bf16[1,8,256,2048]{3,2,0,1:T(8,128)(2,1)}), bf16[1,8,256,2048]{3,2,0,1:T(8,128)(2,1)}, u32[]{:S(2)}, u32[]{:S(2)}) %all-to-all-start) | async-done | bytes 8388640 | tf_op jit(solution)/shard_map/all_to_all | solution.py:45
  944.4 28.0 %copy.47 = bf16[1,1,2048,1408]{3,1,0,2:T(2,128)(2,1)} copy(bf16[1,1,2048,1408]{2,3,1,0:T(8,128)(2,1)} %bitcast.187) | data formatting | bytes 11534336 | tf_op jit(solution)/shard_map/reshape | solution.py:49
  972.9 124.0 %reduce.1 = bf16[2048,1408]{1,0:T(8,128)(2,1)} reduce(bf16[2048,1,1,1408]{3,2,1,0:T(2,128)(2,1)} %bitcast.182, bf16[]{:T(256)} %broadcast.263), dimensions={1,2}, to_apply=%bitcast.51.reduce_sub_computation | reduce | bytes 11534338
  1105.0 202.5 %all-to-all-start.3 = ((bf16[8,2,180224]{2,1,0:T(2,128)(2,1)}), bf16[8,2,180224]{2,1,0:T(2,128)(2,1)}, u32[]{:S(2)}, u32[]{:S(2)}) async-start(bf16[8,2,180224]{2,1,0:T(2,128)(2,1)} %reshape.399), calls=%async_computation.5 | async-start | bytes 11534336 | tf_op jit(solution)/shard_map/all_to_all | solution.py:49
  1307.5 301.4 %conditional.3 = (bf16[1,2048,2048]{2,1,0:T(8,128)(2,1)}) conditional(s32[]{:T(128)} %convert_element_type.551, () %tuple.26, bf16[1,8,256,2048]{3,2,0,1:T(8,128)(2,1)} %all-to-all-done), branch_computations={%region_3.4_spmd, %region_4.5_spmd} | conditional | flops 257991639040 | bytes 293601280 | solution.py:48
  1307.7 22.8 %convolution_convert_fusion.4 = bf16[2048,2048]{1,0:T(8,128)(2,1)S(1)} fusion(bf16[2048,2048]{1,0:T(8,128)(2,1)} %bitcast.1), kind=kOutput, calls=%fused_computation.35 | convolution fusion | flops 17184063488 | bytes 16777216 | tf_op jit(solution)/shard_map/cond/branch_1_fun/brk,bck->brc/dot_general | solution.py:23
  1350.4 23.4 %add_convert_fusion.8 = bf16[2048,2048]{1,0:T(8,128)(2,1)S(1)} fusion(bf16[2048,2048]{1,0:T(8,128)(2,1)} %bitcast.1, bf16[2048,2048]{1,0:T(8,128)(2,1)} %add_convert_fusion.51), kind=kOutput, calls=%fused_computation.8 | convolution fusion | flops 17205035008 | bytes 25165824 | tf_op jit(solution)/shard_map/cond/branch_1_fun/brc,bck->brk/dot_general | solution.py:30
  1624.4 51.1 %reduce = bf16[2048,2048]{1,0:T(8,128)(2,1)} reduce(bf16[2048,1,1,2048]{3,2,1,0:T(2,128)(2,1)} %bitcast.178, bf16[]{:T(256)} %broadcast.263), dimensions={1,2}, to_apply=%bitcast.176.reduce_sub_computation | reduce | bytes 16777218
  1691.7 361.0 %conditional.5 = (bf16[2,1408,2048]{2,1,0:T(8,128)(2,1)}) conditional(s32[]{:T(128)} %convert_element_type.559, () %tuple.28, bf16[2,8,176,2048]{3,2,0,1:T(8,128)(2,1)} %all-to-all-done.4), branch_computations={%region_14.15_spmd, %region_15.16_spmd} | conditional | flops 218561249280 | bytes 389283904 | solution.py:48
  1701.9 25.3 %convolution_convert_fusion.28 = bf16[2,1408,1408]{2,1,0:T(8,128)(2,1)} fusion(bf16[2,1408,2048]{2,1,0:T(8,128)(2,1)} %bitcast.191), kind=kOutput, calls=%fused_computation.109 | convolution fusion | flops 16244310016 | bytes 19464192 | tf_op jit(solution)/shard_map/cond/branch_1_fun/brk,bck->brc/dot_general | solution.py:23
  1748.7 23.1 %add_convert_fusion.38 = bf16[2,1408,2048]{2,1,0:T(8,128)(2,1)} fusion(bf16[2,1408,2048]{2,1,0:T(8,128)(2,1)S(1)} %bitcast.194, bf16[2,1408,1408]{2,1,0:T(8,128)(2,1)} %add_convert_fusion.43.clone.2), kind=kOutput, calls=%fused_computation.94 | convolution fusion | flops 16274948096 | bytes 30998528 | tf_op jit(solution)/shard_map/cond/branch_1_fun/brc,bck->brk/dot_general | solution.py:30
  1771.7 25.1 %convolution_convert_fusion.26 = bf16[2,1408,1408]{2,1,0:T(8,128)(2,1)} fusion(bf16[2,1408,2048]{2,1,0:T(8,128)(2,1)} %add_convert_fusion.38), kind=kOutput, calls=%fused_computation.107 | convolution fusion | flops 16244310016 | bytes 19464192 | tf_op jit(solution)/shard_map/cond/branch_1_fun/brk,bck->brc/dot_general | solution.py:23
  1816.0 26.1 %add_convert_fusion.37 = bf16[2,1408,2048]{2,1,0:T(8,128)(2,1)} fusion(bf16[2,1408,2048]{2,1,0:T(8,128)(2,1)} %add_convert_fusion.38, bf16[2,1408,1408]{2,1,0:T(8,128)(2,1)S(1)} %add_convert_fusion.42.clone.2), kind=kOutput, calls=%fused_computation.93 | convolution fusion | flops 16274948096 | bytes 30998528 | tf_op jit(solution)/shard_map/cond/branch_1_fun/brc,bck->brk/dot_general | solution.py:30
  1842.2 25.2 %convolution_convert_fusion.24 = bf16[2,1408,1408]{2,1,0:T(8,128)(2,1)} fusion(bf16[2,1408,2048]{2,1,0:T(8,128)(2,1)} %add_convert_fusion.37), kind=kOutput, calls=%fused_computation.105 | convolution fusion | flops 16244310016 | bytes 19464192 | tf_op jit(solution)/shard_map/cond/branch_1_fun/brk,bck->brc/dot_general | solution.py:23
  1886.4 25.9 %add_convert_fusion.36 = bf16[2,1408,2048]{2,1,0:T(8,128)(2,1)} fusion(bf16[2,1408,2048]{2,1,0:T(8,128)(2,1)} %add_convert_fusion.37, bf16[2,1408,1408]{2,1,0:T(8,128)(2,1)S(1)} %add_convert_fusion.41.clone.2), kind=kOutput, calls=%fused_computation.92 | convolution fusion | flops 16274948096 | bytes 30998528 | tf_op jit(solution)/shard_map/cond/branch_1_fun/brc,bck->brk/dot_general | solution.py:30
  1912.3 25.1 %convolution_convert_fusion.22 = bf16[2,1408,1408]{2,1,0:T(8,128)(2,1)} fusion(bf16[2,1408,2048]{2,1,0:T(8,128)(2,1)} %add_convert_fusion.36), kind=kOutput, calls=%fused_computation.103 | convolution fusion | flops 16244310016 | bytes 19464192 | tf_op jit(solution)/shard_map/cond/branch_1_fun/brk,bck->brc/dot_general | solution.py:23
  1956.6 25.9 %add_convert_fusion.35 = bf16[2,1408,2048]{2,1,0:T(8,128)(2,1)} fusion(bf16[2,1408,2048]{2,1,0:T(8,128)(2,1)} %add_convert_fusion.36, bf16[2,1408,1408]{2,1,0:T(8,128)(2,1)S(1)} %add_convert_fusion.40.clone.2), kind=kOutput, calls=%fused_computation.91 | convolution fusion | flops 16274948096 | bytes 30998528 | tf_op jit(solution)/shard_map/cond/branch_1_fun/brc,bck->brk/dot_general | solution.py:30
  1982.5 25.2 %convolution_convert_fusion.20 = bf16[2,1408,1408]{2,1,0:T(8,128)(2,1)} fusion(bf16[2,1408,2048]{2,1,0:T(8,128)(2,1)} %add_convert_fusion.35), kind=kOutput, calls=%fused_computation.101 | convolution fusion | flops 16244310016 | bytes 19464192 | tf_op jit(solution)/shard_map/cond/branch_1_fun/brk,bck->brc/dot_general | solution.py:23
  2026.7 25.7 %add_convert_fusion.34 = bf16[2,1408,2048]{2,1,0:T(8,128)(2,1)} fusion(bf16[2,1408,2048]{2,1,0:T(8,128)(2,1)} %add_convert_fusion.35, bf16[2,1408,1408]{2,1,0:T(8,128)(2,1)S(1)} %add_convert_fusion.39.clone.4), kind=kOutput, calls=%fused_computation.90 | convolution fusion | flops 16274948096 | bytes 30998528 | tf_op jit(solution)/shard_map/cond/branch_1_fun/brc,bck->brk/dot_general | solution.py:30
  2130.5 75.7 %all-to-all-done.5 = bf16[2,1,1408,2048]{3,0,1,2:T(2,128)(2,1)} async-done(((bf16[2,1,1408,2048]{3,0,1,2:T(2,128)(2,1)}), bf16[2,1,1408,2048]{3,0,1,2:T(2,128)(2,1)}, u32[]{:S(2)}, u32[]{:S(2)}) %all-to-all-start.5) | async-done | bytes 11534368 | tf_op jit(solution)/shard_map/all_to_all | solution.py:49
  (71 shorter events, 598.6 us)
Async XLA Ops:
  7.2 203.4 %reduce-scatter.4.cloned.1.call-start = ((), (), s32[]{:S(2)}) async-start(), calls=%async_computation.9 | async-start | bytes 37748736 | tf_op jit(solution)/shard_map/reduce_scatter | solution.py:38
  7.9 461.4 %reduce-scatter.8.cloned.1.call-start = ((), (), s32[]{:S(2)}) async-start(), calls=%async_computation.11 | async-start | bytes 51904512 | tf_op jit(solution)/shard_map/reduce_scatter | solution.py:38
  8.7 719.3 %reduce-scatter.6.cloned.1.call-start = ((), (), s32[]{:S(2)}) async-start(), calls=%async_computation.10 | async-start | bytes 51904512 | tf_op jit(solution)/shard_map/reduce_scatter | solution.py:38
  764.1 69.3 %all-to-all-start.2 = ((bf16[1,8,256,1408]{3,2,0,1:T(8,128)(2,1)}), bf16[1,8,256,1408]{3,2,0,1:T(8,128)(2,1)}, u32[]{:S(2)}, u32[]{:S(2)}) async-start(bf16[1,8,256,1408]{3,2,0,1:T(8,128)(2,1)} %pad_bitcast_fusion.1), calls=%async_computation.4 | async-start | bytes 11534336 | tf_op jit(solution)/shard_map/all_to_all | solution.py:45
  833.4 97.7 %all-to-all-start = ((bf16[1,8,256,2048]{3,2,0,1:T(8,128)(2,1)}), bf16[1,8,256,2048]{3,2,0,1:T(8,128)(2,1)}, u32[]{:S(2)}, u32[]{:S(2)}) async-start(bf16[1,8,256,2048]{3,2,0,1:T(8,128)(2,1)} %pad_bitcast_fusion), calls=%async_computation.1 | async-start | bytes 16777216 | tf_op jit(solution)/shard_map/all_to_all | solution.py:45
  931.1 173.9 %all-to-all-start.4 = ((bf16[2,8,176,2048]{3,2,0,1:T(8,128)(2,1)}), bf16[2,8,176,2048]{3,2,0,1:T(8,128)(2,1)}, u32[]{:S(2)}, u32[]{:S(2)}) async-start(bf16[2,8,176,2048]{3,2,0,1:T(8,128)(2,1)} %copy.48), calls=%async_computation.7 | async-start | bytes 23068672 | tf_op jit(solution)/shard_map/all_to_all | solution.py:45
  1105.0 581.7 %all-to-all-start.3 = ((bf16[8,2,180224]{2,1,0:T(2,128)(2,1)}), bf16[8,2,180224]{2,1,0:T(2,128)(2,1)}, u32[]{:S(2)}, u32[]{:S(2)}) async-start(bf16[8,2,180224]{2,1,0:T(2,128)(2,1)} %reshape.399), calls=%async_computation.5 | async-start | bytes 11534336 | tf_op jit(solution)/shard_map/all_to_all | solution.py:49
  1686.7 387.8 %all-to-all-start.1 = ((bf16[8,2,262144]{2,1,0:T(2,128)(2,1)}), bf16[8,2,262144]{2,1,0:T(2,128)(2,1)}, u32[]{:S(2)}, u32[]{:S(2)}) async-start(bf16[8,2,262144]{2,1,0:T(2,128)(2,1)} %reshape.397), calls=%async_computation.2 | async-start | bytes 16777216 | tf_op jit(solution)/shard_map/all_to_all | solution.py:49
  1701.9 46.8 %slice-start = ((s8[11534336]{0:T(1024)(128)(4,1)}), s8[3145728]{0:T(1024)(128)(4,1)S(1)}, s32[]{:S(2)}) async-start(s8[11534336]{0:T(1024)(128)(4,1)} %bitcast.192), calls=%async_computation.12 | async-start | bytes 6291456 | tf_op jit(solution)/shard_map/cond
  1701.9 46.8 %slice-start.1 = ((s8[11534336]{0:T(1024)(128)(4,1)}), s8[4194304]{0:T(1024)(128)(4,1)S(1)}, s32[]{:S(2)}) async-start(s8[11534336]{0:T(1024)(128)(4,1)} %bitcast.192), calls=%async_computation.13 | async-start | bytes 8388608 | tf_op jit(solution)/shard_map/cond
  1727.1 21.5 slice-start.2
  2074.5 131.7 %all-to-all-start.5 = ((bf16[2,1,1408,2048]{3,0,1,2:T(2,128)(2,1)}), bf16[2,1,1408,2048]{3,0,1,2:T(2,128)(2,1)}, u32[]{:S(2)}, u32[]{:S(2)}) async-start(bf16[2,1,1408,2048]{3,0,1,2:T(2,128)(2,1)} %bitcast.181), calls=%async_computation.8 | async-start | bytes 23068672 | tf_op jit(solution)/shard_map/all_to_all | solution.py:49
  2114.9 11.9 copy-start
Sparse Core Ops, SparseCore 0:
  11.5 199.0 reduce-scatter.3
  214.1 255.1 reduce-scatter.7
  472.8 255.0 reduce-scatter.5
where the time goes:
time: 2240 us; the launch traced here: 2230 us
  waiting for transfers between devices  915 us (41%)
  matrix products  651 us (29%)
  other arithmetic  227 us (10%)
  starting transfers between devices  221 us (10%)
  local copies, waits for them, and re-layouts  170 us (8%)
    reduce_scatter x3, waiting for transfers between devices, stack_step(): lax.psum_scatter(grad_all[0], 'data', scatter_dimension=1, tiled=True)  704 us
    dot_general x10, matrix products, newton_schulz(): jnp.einsum('brc,bck->brk', poly_mat, x_mat, preferred_element_type=jnp.fl...  232 us
    dot_general x10, matrix products, newton_schulz(): jnp.einsum('brk,bck->brc', x_mat, x_mat, preferred_element_type=jnp.float32)  222 us
    all_to_all x3, starting transfers between devices, stack_step(): lax.all_to_all(ortho_mat.reshape(slots, 1, n_rows, n_cols), 'data', 2, 1,...  210 us
    dot_general x10, matrix products, newton_schulz(): jnp.einsum('brk,bkc->brc', gram_mat, gram_mat, preferred_element_type=jnp...  197 us
    unnamed x2, other arithmetic  175 us
    all_to_all x3, waiting for transfers between devices, stack_step(): lax.all_to_all(send_buf, 'data', 1, 2, tiled=True)  134 us
    all_to_all x3, waiting for transfers between devices, stack_step(): lax.all_to_all(ortho_mat.reshape(slots, 1, n_rows, n_cols), 'data', 2, 1,...  75.7 us
  transfers between devices with their start and end apart: 9, of which 6 were waited for; matrix products, arithmetic and copies ran while one was open for 46% of the time, Pallas kernels for 0%

commit v1 on v0

v1 whole, which is shorter than its diff:
```python
import math
import functools
import jax
import jax.numpy as jnp
from jax import lax
from jax.experimental import pallas as pl
from jax.experimental.pallas import tpu as pltpu
from jax.experimental.layout import Layout, with_layout_constraint
from jax.sharding import PartitionSpec as P

MOMENTUM = 0.95
LEARN_RATE = 0.25
WEIGHT_DECAY = 0.2
EPSILON = 1e-7
COEF_A = 3.4445
COEF_B = -4.7750
COEF_C = 2.0315
NS_STEPS = 5
GROUP = 8
FIRST_JOBS = ((0, 0, 0, 0), (0, 1, 3, 0), (1, 0, 1, 0), (1, 2, 2, 0), (1, 1, 1, 1), (1, 3, 2, 1))
LAST_JOBS = ((0, 0, 0, 0), (0, 1, 1, 0), (0, 2, 2, 0), (0, 3, 3, 0))


def greet_all(me):
    barrier = pltpu.get_barrier_semaphore()
    for step in range(1, GROUP):
        pl.semaphore_signal(barrier, inc=1, device_id={'data': lax.rem(me + step, GROUP)}, device_id_type=pl.DeviceIdType.MESH)
    pl.semaphore_wait(barrier, GROUP - 1)


def share_kernel(part_ref, all_ref, send_sem, recv_sem):
    me = lax.axis_index('data')
    greet_all(me)
    copies = []
    for step in range(1, GROUP):
        copies.append(pltpu.make_async_remote_copy(
            src_ref=part_ref, dst_ref=all_ref.at[step], send_sem=send_sem.at[step], recv_sem=recv_sem.at[step],
            device_id={'data': lax.rem(me + step, GROUP)}, device_id_type=pl.DeviceIdType.MESH))
    for copy in copies:
        copy.start()
    all_ref[0] = part_ref[...]
    for copy in copies:
        copy.wait()


def sum_over_data(partial, collective_id):
    count = partial.shape[0]
    tile = jnp.broadcast_to(jnp.pad(partial, (0, 8 - count))[:, None], (8, 128))
    shared = pl.pallas_call(
        share_kernel,
        out_shape=jax.ShapeDtypeStruct((GROUP, 8, 128), jnp.float32),
        in_specs=[pl.BlockSpec(memory_space=pltpu.VMEM)],
        out_specs=pl.BlockSpec(memory_space=pltpu.VMEM),
        scratch_shapes=[pltpu.SemaphoreType.DMA((GROUP,)), pltpu.SemaphoreType.DMA((GROUP,))],
        compiler_params=pltpu.CompilerParams(collective_id=collective_id, has_side_effects=True),
        cost_estimate=pl.CostEstimate(flops=20_000_000, bytes_accessed=65536, transcendentals=0),
        name=f'share{collective_id}',
    )(tile)
    me = lax.axis_index('data')
    ordered = jnp.take(shared[:, :, 0], lax.rem(me - jnp.arange(GROUP) + GROUP, GROUP), axis=0)
    return jnp.sum(ordered, axis=0)[:count]


def block_of(ref, device, size, axis):
    start = pl.multiple_of(device * size, size)
    return ref.at[pl.ds(start, size), :] if axis == 0 else ref.at[:, pl.ds(start, size)]


def ortho_kernel(jobs, *refs):
    n_stacks = 1 + max(job[0] for job in jobs)
    ins, outs = refs[:n_stacks], refs[n_stacks:2 * n_stacks]
    (x_ref, a_ref, b_ref, send_sem, recv_sem, pass_sem, passed_sem, back_sem, got_sem, own_sem, tile_send, tile_recv) = refs[2 * n_stacks:]
    me = lax.axis_index('data')
    chip, core = me // 2, me % 2
    partner = me + 1 - 2 * core
    greet_all(me)
    n_long = x_ref.shape[3]
    chips = GROUP // 2
    last = NS_STEPS % 2

    def remote(src, dst, send, recv, target):
        return pltpu.make_async_remote_copy(src_ref=src, dst_ref=dst, send_sem=send, recv_sem=recv,
                                            device_id={'data': target}, device_id_type=pl.DeviceIdType.MESH)

    def block(job, slot, device):
        _, _, _, turn, axis, n_short = jobs[job]
        size = (n_short if axis == 0 else n_long) // GROUP
        return block_of(x_ref.at[turn, slot, pl.ds(0, n_short)], device, size, axis)

    def rows_in(job):
        return ins[jobs[job][0]].at[jobs[job][1]]

    def rows_out(job):
        return outs[jobs[job][0]].at[jobs[job][1]]

    def collect(job, source):
        return remote(rows_in(job), block(job, 0, 2 * source + core), send_sem.at[job], recv_sem.at[job, source], 2 * jobs[job][2] + core)

    def collect_own(job):
        return pltpu.make_async_copy(rows_in(job), block(job, 0, me), own_sem.at[job])

    def pass_on(job, source, side):
        there = block(job, 0, 2 * source + side)
        return remote(there, there, pass_sem.at[job, source], passed_sem.at[job, source], partner)

    def hand_out(job, target):
        return remote(block(job, last, 2 * target + core), rows_out(job), back_sem.at[job, target], got_sem.at[job], 2 * target + core)

    def hand_out_own(job):
        return pltpu.make_async_copy(block(job, last, me), rows_out(job), own_sem.at[job])

    for job, (_, _, owner, turn, _, n_short) in enumerate(jobs):
        @pl.when(chip != owner)
        def _():
            collect(job, chip).start()

        @pl.when(chip == owner)
        def _():
            collect_own(job).start()
            n_pad = padded(n_short)
            if n_pad > n_short:
                for slot in range(2):
                    x_ref[turn, slot, n_short:n_pad, :] = jnp.zeros((n_pad - n_short, n_long), jnp.bfloat16)

    for turn in range(x_ref.shape[0]):
        mine = [job for job in range(len(jobs)) if jobs[job][3] == turn]
        for job in mine:
            owner = jobs[job][2]

            @pl.when(chip == owner)
            def _():
                collect_own(job).wait()
                pass_on(job, owner, core).start()
                for source in range(chips):
                    if source != owner:
                        collect(job, source).wait_recv()
                        pass_on(job, source, core).start()
                for source in range(chips):
                    pass_on(job, source, core).wait_send()
                    pass_on(job, source, 1 - core).wait_recv()
        for n_short in sorted({jobs[job][5] for job in mine}):
            @pl.when(functools.reduce(jnp.logical_or, [chip == jobs[job][2] for job in mine if jobs[job][5] == n_short]))
            def _():
                n_pad = padded(n_short)
                square = pl.ds(0, n_pad)
                step = functools.partial(ns_step, n_short, core, partner, remote, x_ref.at[turn, :, pl.ds(0, n_pad)],
                                         a_ref.at[square, square], b_ref.at[square, square], tile_send, tile_recv)
                lax.fori_loop(0, NS_STEPS, step, 0)
        for job in mine:
            owner = jobs[job][2]

            @pl.when(chip == owner)
            def _():
                for target in range(chips):
                    (hand_out_own(job) if target == owner else hand_out(job, target)).start()

    for job, (_, _, owner, _, _, _) in enumerate(jobs):
        @pl.when(chip == owner)
        def _():
            hand_out_own(job).wait()
            for target in range(chips):
                if target != owner:
                    hand_out(job, target).wait_send()

        @pl.when(chip != owner)
        def _():
            collect(job, chip).wait_send()
            hand_out(job, chip).wait_recv()


def padded(n_short):
    return -(-n_short // TILE) * TILE


TILE = 512


def ns_step(n_short, core, partner, remote, x_ref, a_ref, b_ref, tile_send, tile_recv, step, carry):
    n_pad, n_long = x_ref.shape[1:]
    x_now, x_next = x_ref.at[step % 2], x_ref.at[(step + 1) % 2]
    tiles = n_pad // TILE

    def span(i, length=TILE):
        return pl.ds(pl.multiple_of(i * length, length), length)

    def send(stage, ref):
        remote(ref, ref, tile_send.at[stage], tile_recv.at[stage], partner).start()

    def await_tiles(stage, sent, received):
        def view(count):
            return x_ref.at[0, pl.ds(0, count * TILE * TILE // n_long), :]
        for side in range(2):
            @pl.when(core == side)
            def _():
                remote(view(sent[side]), view(sent[side]), tile_send.at[stage], tile_recv.at[stage], partner).wait_send()
                remote(view(received[side]), view(received[side]), tile_send.at[stage], tile_recv.at[stage], partner).wait_recv()

    def owner_of(i, j):
        return (i // 2 + j) % 2

    def upper(stage, ref, body):
        def visit(t, c):
            i, j = t // tiles, t % tiles

            @pl.when(jnp.logical_and(i <= j, owner_of(i, j) == core))
            def _():
                tile = body(i, j)
                ref[span(i), span(j)] = tile
                send(stage, ref.at[span(i), span(j)])

                @pl.when(i != j)
                def _():
                    ref[span(j), span(i)] = tile.T
                    send(stage, ref.at[span(j), span(i)])
            return c
        lax.fori_loop(0, tiles * tiles, visit, 0)
        count = [sum(1 + (i != j) for i in range(tiles) for j in range(i, tiles) if owner_of(i, j) == side) for side in range(2)]
        await_tiles(stage, count, count[::-1])

    def gram(i, j):
        tile = lax.dot_general(x_now[span(i), :], x_now[span(j), :], (((1,), (1,)), ((), ())), preferred_element_type=jnp.float32)
        return tile.astype(jnp.bfloat16)

    def poly(i, j):
        square = jnp.dot(a_ref[span(i), :n_short], a_ref[:n_short, span(j)], preferred_element_type=jnp.float32)
        tile = COEF_B * a_ref[span(i), span(j)].astype(jnp.float32) + COEF_C * square.astype(jnp.bfloat16).astype(jnp.float32)
        return tile.astype(jnp.bfloat16)

    upper(0, a_ref, gram)
    upper(1, b_ref, poly)
    height = n_short // 2
    wide = n_long // TILE // 2

    def apply(t, c):
        rows, cols = span(t // wide, height), span(core * wide + t % wide)
        update = jnp.dot(b_ref[rows, :n_short], x_now[:n_short, cols], preferred_element_type=jnp.float32).astype(jnp.bfloat16)
        x_next[rows, cols] = (COEF_A * x_now[rows, cols].astype(jnp.float32) + update.astype(jnp.float32)).astype(jnp.bfloat16)
        send(2, x_next.at[rows, cols])
        return c

    lax.fori_loop(0, 2 * wide, apply, 0)
    half = x_ref.at[0, pl.ds(0, n_short // 2), :]
    remote(half, half, tile_send.at[2], tile_recv.at[2], partner).wait()
    return carry


def orthogonalize(jobs, stacks, collective_id):
    shorts = [rows.shape[1] * (GROUP if axis == 0 else 1) for rows, axis in stacks]
    n_long = stacks[0][0].shape[2] * (GROUP if stacks[0][1] == 1 else 1)
    full = [(stack, k, chip, turn, stacks[stack][1], shorts[stack]) for stack, k, chip, turn in jobs]
    n_pad = padded(max(shorts))
    turns = 1 + max(job[3] for job in jobs)
    n_jobs, chips = len(jobs), GROUP // 2
    dma = pltpu.SemaphoreType.DMA
    return pl.pallas_call(
        functools.partial(ortho_kernel, full),
        out_shape=[jax.ShapeDtypeStruct(rows.shape, rows.dtype) for rows, _ in stacks],
        in_specs=[pl.BlockSpec(memory_space=pl.ANY)] * len(stacks),
        out_specs=[pl.BlockSpec(memory_space=pl.ANY)] * len(stacks),
        scratch_shapes=[pltpu.VMEM((turns, 2, n_pad, n_long), jnp.bfloat16), pltpu.VMEM((n_pad, n_pad), jnp.bfloat16),
                        pltpu.VMEM((n_pad, n_pad), jnp.bfloat16),
                        dma((n_jobs,)), dma((n_jobs, chips)), dma((n_jobs, chips)), dma((n_jobs, chips)), dma((n_jobs, chips)),
                        dma((n_jobs,)), dma((n_jobs,)), dma((3,)), dma((3,))],
        compiler_params=pltpu.CompilerParams(collective_id=collective_id, has_side_effects=True, vmem_limit_bytes=58 << 20),
        cost_estimate=pl.CostEstimate(flops=2_000_000_000, bytes_accessed=16 << 20, transcendentals=0),
        name=f'ortho{collective_id}',
    )(*[rows for rows, _ in stacks])


SLOTS = 5


def reduce_kernel(n_chunks, per_matrix, grad_ref, out_ref, own_ref, pair_ref, first_ref, second_ref, sum_ref,
                  load_sem, pair_send, pair_recv, first_send, first_recv, second_send, second_recv, out_sem):
    me = lax.axis_index('data')
    y, x, core = me // 4, (me // 2) % 2, me % 2
    greet_all(me)
    chunk = own_ref.shape[3]
    half = chunk // 2
    parts = (pl.ds(0, half), pl.ds(half, half))
    over_core, over_x, over_y = me + 1 - 2 * core, me + 2 - 4 * x, me + 4 - 8 * y

    def remote(src, dst, send, recv, target):
        return pltpu.make_async_remote_copy(src_ref=src, dst_ref=dst, send_sem=send, recv_sem=recv,
                                            device_id={'data': target}, device_id_type=pl.DeviceIdType.MESH)

    def rows_of(c):
        return pl.ds(pl.multiple_of((c % per_matrix) * chunk, chunk), chunk)

    def load(c):
        return pltpu.make_async_copy(grad_ref.at[c // per_matrix, :, :, core, rows_of(c)], own_ref.at[c % SLOTS], load_sem.at[c % SLOTS])

    def pair(c):
        return remote(grad_ref.at[c // per_matrix, :, :, 1 - core, rows_of(c)], pair_ref.at[c % SLOTS],
                      pair_send.at[c % SLOTS], pair_recv.at[c % SLOTS], over_core)

    def first(c):
        slot = c % SLOTS
        return (remote(own_ref.at[slot, :, 1 - x, parts[0]], first_ref.at[slot, 0], first_send.at[slot, 0], first_recv.at[slot, 0], over_x),
                remote(own_ref.at[slot, 1 - y, :, parts[1]], first_ref.at[slot, 1], first_send.at[slot, 1], first_recv.at[slot, 1], over_y))

    def second(c):
        slot = c % SLOTS
        return (remote(own_ref.at[slot, 1 - y, x, parts[0]], second_ref.at[slot, 0], second_send.at[slot, 0], second_recv.at[slot, 0], over_y),
                remote(own_ref.at[slot, y, 1 - x, parts[1]], second_ref.at[slot, 1], second_send.at[slot, 1], second_recv.at[slot, 1], over_x))

    def store(c):
        return pltpu.make_async_copy(sum_ref.at[c % SLOTS], out_ref.at[c // per_matrix, rows_of(c)], out_sem.at[c % SLOTS])

    def during(c, body):
        pl.when(jnp.logical_and(c >= 0, c < n_chunks))(lambda: body(c))

    def finish(c):
        slot = c % SLOTS
        for copy in second(c):
            copy.wait()
        pl.when(c >= SLOTS)(lambda: store(c - SLOTS).wait())
        for side in range(2):
            sum_ref[slot, parts[side]] = own_ref[slot, y, x, parts[side]] + second_ref[slot, side]
        store(c).start()

    def middle(c):
        slot = c % SLOTS
        for copy in first(c):
            copy.wait()
        for other in range(2):
            own_ref[slot, other, x, parts[0]] += first_ref[slot, 0, other]
            own_ref[slot, y, other, parts[1]] += first_ref[slot, 1, other]
        for copy in second(c):
            copy.start()

    def begin(c):
        slot = c % SLOTS
        load(c).wait()
        pair(c).wait()
        own_ref[slot] += pair_ref[slot]
        for copy in first(c):
            copy.start()

    def fetch(c):
        load(c).start()
        pair(c).start()

    def visit(t, carry):
        during(t - 5, finish)
        during(t - 3, middle)
        during(t - 1, begin)
        during(t, fetch)
        return carry

    lax.fori_loop(0, n_chunks + 5, visit, 0)
    for c in range(max(0, n_chunks - SLOTS), n_chunks):
        store(c).wait()


def reduce_rows_kernel(grad, chunk, collective_id):
    count, n_rows, n_cols = grad.shape
    rows = n_rows // GROUP
    per_matrix = rows // chunk
    dma, vmem = pltpu.SemaphoreType.DMA, lambda *shape: pltpu.VMEM(shape, jnp.float32)
    return pl.pallas_call(
        functools.partial(reduce_kernel, count * per_matrix, per_matrix),
        out_shape=jax.ShapeDtypeStruct((count, rows, n_cols), jnp.float32),
        in_specs=[pl.BlockSpec(memory_space=pl.ANY)],
        out_specs=pl.BlockSpec(memory_space=pl.ANY),
        scratch_shapes=[vmem(SLOTS, 2, 2, chunk, n_cols), vmem(SLOTS, 2, 2, chunk, n_cols), vmem(SLOTS, 2, 2, chunk // 2, n_cols),
                        vmem(SLOTS, 2, chunk // 2, n_cols), vmem(SLOTS, chunk, n_cols),
                        dma((SLOTS,)), dma((SLOTS,)), dma((SLOTS,)), dma((SLOTS, 2)), dma((SLOTS, 2)), dma((SLOTS, 2)), dma((SLOTS, 2)),
                        dma((SLOTS,))],
        compiler_params=pltpu.CompilerParams(collective_id=collective_id, has_side_effects=True, vmem_limit_bytes=40 << 20),
        cost_estimate=pl.CostEstimate(flops=1_000_000_000, bytes_accessed=64 << 20, transcendentals=0),
        name=f'reduce{collective_id}',
    )(grad.reshape(count, 2, 2, 2, rows, n_cols))


def momentum(grad_rows, mom_old):
    mom_new = MOMENTUM * mom_old + grad_rows / GROUP
    return mom_new, jnp.sum(mom_new * mom_new, axis=(1, 2))


def to_send(mom_new, norm_sq, transposed):
    x_rows = (mom_new / (jnp.sqrt(norm_sq)[:, None, None] + EPSILON)).astype(jnp.bfloat16)
    return jnp.swapaxes(x_rows, 1, 2) if transposed else x_rows


def new_weights(ortho_rows, master_old, n_rows, n_cols):
    scale = 0.2 * math.sqrt(max(n_rows, n_cols))
    master_new = master_old - LEARN_RATE * (scale * ortho_rows.astype(jnp.float32) + WEIGHT_DECAY * master_old)
    return master_new, master_new.astype(jnp.bfloat16)


def solution(mesh):
    grad_spec = P(('stage', 'data'), None, None, None)
    row_spec = P('stage', 'data', None)

    def step_local(g_attn, m_attn, w_attn, g_up, m_up, w_up, g_down, m_down, w_down):
        def reduce_rows(grad):
            return lax.psum_scatter(grad[0], 'data', scatter_dimension=1, tiled=True)

        r_attn = reduce_rows(g_attn)
        r_down = reduce_rows(g_down)
        r_up = reduce_rows_kernel(g_up[0], 32, 7)
        r_attn, r_up = lax.optimization_barrier((r_attn, r_up))

        mn_attn, part_attn = momentum(r_attn, m_attn)
        mn_up, part_up = momentum(r_up, m_up)
        mn_up = with_layout_constraint(mn_up, Layout((0, 1, 2)))
        parts = sum_over_data(jnp.concatenate([part_attn, part_up]), 0)
        x_attn = to_send(mn_attn, parts[:2], False)
        x_up = to_send(mn_up, parts[2:], True)
        or_attn, or_up = orthogonalize(FIRST_JOBS, [(x_attn, 0), (x_up, 1)], 1)
        wn_attn, wb_attn = new_weights(or_attn, w_attn, 2048, 2048)
        wn_up, wb_up = new_weights(jnp.swapaxes(or_up, 1, 2), w_up, 2048, 1408)

        r_down, wn_attn, wb_attn, wn_up, wb_up = lax.optimization_barrier((r_down, wn_attn, wb_attn, wn_up, wb_up))
        mn_down, part_down = momentum(r_down, m_down)
        x_down = to_send(mn_down, sum_over_data(part_down, 4), False)
        or_down, = orthogonalize(LAST_JOBS, [(x_down, 0)], 5)
        wn_down, wb_down = new_weights(or_down, w_down, 1408, 2048)
        return (mn_attn, wn_attn, wb_attn, mn_up, wn_up, wb_up, mn_down, wn_down, wb_down)

    in_specs = (grad_spec, row_spec, row_spec) * 3
    out_specs = (row_spec,) * 9
    return jax.shard_map(step_local, mesh=mesh, in_specs=in_specs, out_specs=out_specs, check_vma=False)
```

time: 2240 us -> 928 us (0.41)
  waiting for transfers between devices: 915 us -> 1.4 us
  Pallas kernels: 0 us -> 831 us
  matrix products: 651 us -> 0 us
  starting transfers between devices: 221 us -> 0.08 us
  other arithmetic: 227 us -> 52.5 us
  local copies, waits for them, and re-layouts: 170 us -> 28 us
    pallas_call x0 -> x5, Pallas kernels: none -> 831 us  [the longest x2 487 us: orthogonalize(): pl.pallas_call(functools.partial(ortho_kernel, full), out_shape=[jax.Shap...]
    reduce_scatter x3 -> x2, waiting for transfers between devices: 704 us -> 0.02 us  [reduce_rows(): return lax.psum_scatter(grad[0], 'data', scatter_dimension=1, tiled=True)]
    dot_general x30 -> x0, matrix products: 651 us -> none  [the longest x10 232 us: newton_schulz(): jnp.einsum('brc,bck->brk', poly_mat, x_mat, preferred_element_type=jnp.fl...]
    all_to_all x6 -> x0, starting transfers between devices: 221 us -> none  [the longest x3 210 us: stack_step(): lax.all_to_all(ortho_mat.reshape(slots, 1, n_rows, n_cols), 'data', 2, 1,...]
    all_to_all x6 -> x0, waiting for transfers between devices: 210 us -> none  [the longest x3 134 us: stack_step(): lax.all_to_all(send_buf, 'data', 1, 2, tiled=True)]
    unnamed x2 -> x1, other arithmetic: 175 us -> 0.01 us
    reshape x5 -> x0, local copies, waits for them, and re-layouts: 60.6 us -> none  [the longest x2 43.5 us: stack_step(): ortho_mat.reshape(slots, 1, n_rows, n_cols)]
    unnamed x9 -> x15, local copies, waits for them, and re-layouts: 60.6 us -> 17.7 us
  transfers between devices with their start and end apart: 9 -> 2, of which waited for: 6 -> 0; matrix products, arithmetic and copies ran while one was open for 46% -> 5% of each run, Pallas kernels for 0% -> 70%
where the time goes in v1:
time: 928 us; the launch traced here: 927 us
  Pallas kernels  831 us (90%)
  other arithmetic  52.5 us (6%)
  local copies, waits for them, and re-layouts  28 us (3%)
  between operations  14.2 us (2%)
    pallas_call x2, Pallas kernels, orthogonalize(): pl.pallas_call(functools.partial(ortho_kernel, full), out_shape=[jax.Shap...  487 us
    pallas_call x1, Pallas kernels, reduce_rows_kernel(): pl.pallas_call(functools.partial(reduce_kernel, count * per_matrix, per_m...  330 us
    reduce_sum x3, other arithmetic, momentum(): return (mom_new, jnp.sum(mom_new * mom_new, axis=(1, 2)))  22.8 us
  transfers between devices with their start and end apart: 2, of which 0 were waited for; matrix products, arithmetic and copies ran while one was open for 5% of the time, Pallas kernels for 70%

profile of v1, /device:TPU:0, one launch (start us, length us, event | category | flops | bytes accessed | tf_op | source)
XLA Modules:
  0.0 926.8 jit_solution(17572245753178600233)
XLA Ops:
  7.2 0.7 reduce-scatter.3.cloned.1.call-update
  8.0 0.7 reduce-scatter.5.cloned.1.call-update
  8.7 6.2 copy.25
  14.9 329.8 %reduce7.1 = f32[4,256,1408]{2,1,0:T(8,128)S(1)} custom-call(f32[4,2,2,2,256,1408]{5,4,3,2,1,0:T(8,128)} %bitcast.12), custom_call_target="tpu_custom_call" | custom-call | flops 1000000000 | bytes 67108864 | tf_op jit(solution)/shard_map/reduce7/pallas_call | solution.py:361
  344.7 2.5 copy-done
  347.3 7.8 multiply_reduce_fusion.1
  355.2 6.2 copy.23
  361.4 6.6 multiply_reduce_fusion.2
  368.1 0.7 broadcast_in_dim.13.part_ref
  368.8 6.1 share0.1
  374.8 0.8 slice_reduce_fusion.1
  376.4 4.2 divide_convert_fusion.2.refs_0_
  380.6 2.2 fusion.2.refs_1_
  382.9 315.5 %ortho1.1 = (bf16[2,256,2048]{2,1,0:T(8,128)(2,1)}, bf16[4,1408,256]{2,1,0:T(8,128)(2,1)}) custom-call(bf16[2,256,2048]{2,1,0:T(8,128)(2,1)} %divide_convert_fusion.2.refs_0_, bf16[4,1408,256]{2,1,0:T(8,128)(2,1)} %fusion.2.refs_1_), custom_call_target="tpu_custom_call" | custom-call | flops 2000000000 | bytes 16777216 | tf_op jit(solution)/shard_map/ortho1/pallas_call | solution.py:255
  698.4 5.6 fusion.8
  704.0 3.8 fusion.6
  707.8 2.7 copy.27
  710.5 6.2 copy.26
  716.7 8.3 multiply_reduce_fusion
  725.7 8.1 share4.1
  733.8 0.8 slice_reduce_fusion
  735.3 5.0 divide_convert_fusion.refs_0_
  740.3 171.1 %ortho5.1 = bf16[4,176,2048]{2,1,0:T(8,128)(2,1)} custom-call(bf16[4,176,2048]{2,1,0:T(8,128)(2,1)} %divide_convert_fusion.refs_0_), custom_call_target="tpu_custom_call" | custom-call | flops 2000000000 | bytes 16777216 | tf_op jit(solution)/shard_map/ortho5/pallas_call | solution.py:255
  911.4 8.6 fusion.5
  (29 shorter events, 2.3 us)
Async XLA Ops:
  7.2 340.1 %reduce-scatter.3.cloned.1.call-start = ((), (), s32[]{:S(2)}) async-start(), calls=%async_computation.2 | async-start | bytes 37748736 | tf_op jit(solution)/shard_map/reduce_scatter | solution.py:398
  7.9 699.9 %reduce-scatter.5.cloned.1.call-start = ((), (), s32[]{:S(2)}) async-start(), calls=%async_computation.3 | async-start | bytes 51904512 | tf_op jit(solution)/shard_map/reduce_scatter | solution.py:398
  344.7 2.5 copy-start
  376.2 4.4 copy-start.1
  382.9 315.5 %copy-start.2 = (f32[2,256,2048]{2,1,0:T(8,128)S(1)}, f32[2,256,2048]{2,1,0:T(8,128)}, u32[]{:S(2)}) copy-start(f32[2,256,2048]{2,1,0:T(8,128)} %param.13) | copy-start | bytes 12582916
  382.9 321.1 %slice-start = ((s8[5767168]{0:T(1024)(128)(4,1)}), s8[1572864]{0:T(1024)(128)(4,1)S(1)}, s32[]{:S(2)}) async-start(s8[5767168]{0:T(1024)(128)(4,1)} %bitcast.15), calls=%async_computation.4 | async-start | bytes 3145728
  698.4 5.6 slice-start.1
  698.4 5.6 copy-start.3
Sparse Core Ops, SparseCore 0:
  11.5 333.9 reduce-scatter.2
  349.0 346.4 reduce-scatter.4

commit v2 on v1

--- a/solution.py
+++ b/solution.py
@@ -5,7 +5,6 @@
 from jax import lax
 from jax.experimental import pallas as pl
 from jax.experimental.pallas import tpu as pltpu
-from jax.experimental.layout import Layout, with_layout_constraint
 from jax.sharding import PartitionSpec as P
 
 MOMENTUM = 0.95
@@ -66,16 +65,23 @@
     return ref.at[pl.ds(start, size), :] if axis == 0 else ref.at[:, pl.ds(start, size)]
 
 
-def ortho_kernel(jobs, *refs):
+def ortho_kernel(jobs, late, keep, *refs):
     n_stacks = 1 + max(job[0] for job in jobs)
-    ins, outs = refs[:n_stacks], refs[n_stacks:2 * n_stacks]
-    (x_ref, a_ref, b_ref, send_sem, recv_sem, pass_sem, passed_sem, back_sem, got_sem, own_sem, tile_send, tile_recv) = refs[2 * n_stacks:]
+    n_late = 1 + max([job[0] for job in late], default=-1)
+    n_in = n_stacks + (n_late > 0)
+    n_out = 1 if keep else n_stacks
+    ins, kept_in = refs[:n_stacks], refs[n_in - 1]
+    outs, late_outs = refs[n_in:n_in + n_out], refs[n_in + n_out:n_in + n_out + n_late]
+    scratch = refs[n_in + n_out + n_late:]
+    (x_ref, a_ref, b_ref, far_ref, send_sem, recv_sem, pass_sem, passed_sem, back_sem, got_sem, own_sem,
+     tile_send, tile_recv) = scratch[:13]
     me = lax.axis_index('data')
     chip, core = me // 2, me % 2
     partner = me + 1 - 2 * core
     greet_all(me)
-    n_long = x_ref.shape[3]
+    n_long = x_ref.shape[1]
     chips = GROUP // 2
+    turn_rows = rows_of_turn(jobs, 0)
     last = NS_STEPS % 2
 
     def remote(src, dst, send, recv, target):
@@ -85,7 +91,7 @@
     def block(job, slot, device):
         _, _, _, turn, axis, n_short = jobs[job]
         size = (n_short if axis == 0 else n_long) // GROUP
-        return block_of(x_ref.at[turn, slot, pl.ds(0, n_short)], device, size, axis)
+        return block_of(x_ref.at[pl.ds(turn * turn_rows + slot * padded(n_short), n_short)], device, size, axis)
 
     def rows_in(job):
         return ins[jobs[job][0]].at[jobs[job][1]]
@@ -108,6 +114,50 @@
 
     def hand_out_own(job):
         return pltpu.make_async_copy(block(job, last, me), rows_out(job), own_sem.at[job])
+
+    def store(job):
+        _, _, _, turn, _, n_short = jobs[job]
+        there = x_ref.at[pl.ds(turn * turn_rows + last * padded(n_short), n_short)]
+        return pltpu.make_async_copy(there, outs[0].at[pl.ds(turn * n_short, n_short)], own_sem.at[job])
+
+    def late_block(index, device):
+        _, _, _, turn, axis, n_short = late[index]
+        size = (n_short if axis == 0 else n_long) // GROUP
+        return block_of(kept_in.at[pl.ds(turn * n_short, n_short)], device, size, axis)
+
+    def late_out(index):
+        return late_outs[late[index][0]].at[late[index][1]]
+
+    def late_hand_out(index, target):
+        return remote(late_block(index, 2 * target + core), late_out(index), scratch[13].at[index, target], scratch[14].at[index], 2 * target + core)
+
+    def late_own(index, outward):
+        room = scratch[16 + late[index][0]].at[late[index][3]]
+        if outward:
+            return pltpu.make_async_copy(room, late_out(index), scratch[15].at[index, 1])
+        return pltpu.make_async_copy(late_block(index, me), room, scratch[15].at[index, 0])
+
+    def each_late(owning, other=None):
+        for index, job in enumerate(late):
+            pl.when(chip == job[2])(functools.partial(owning, index))
+            if other is not None:
+                pl.when(chip != job[2])(functools.partial(other, index))
+
+    def late_begin(index):
+        late_own(index, False).start()
+        for target in range(chips):
+            if target != late[index][2]:
+                late_hand_out(index, target).start()
+
+    def late_middle(index):
+        late_own(index, False).wait()
+        late_own(index, True).start()
+
+    def late_end(index):
+        late_own(index, True).wait()
+        for target in range(chips):
+            if target != late[index][2]:
+                late_hand_out(index, target).wait_send()
 
     for job, (_, _, owner, turn, _, n_short) in enumerate(jobs):
         @pl.when(chip != owner)
@@ -120,43 +170,52 @@
             n_pad = padded(n_short)
             if n_pad > n_short:
                 for slot in range(2):
-                    x_ref[turn, slot, n_short:n_pad, :] = jnp.zeros((n_pad - n_short, n_long), jnp.bfloat16)
-
-    for turn in range(x_ref.shape[0]):
-        mine = [job for job in range(len(jobs)) if jobs[job][3] == turn]
-        for job in mine:
-            owner = jobs[job][2]
-
-            @pl.when(chip == owner)
-            def _():
-                collect_own(job).wait()
-                pass_on(job, owner, core).start()
-                for source in range(chips):
-                    if source != owner:
-                        collect(job, source).wait_recv()
-                        pass_on(job, source, core).start()
-                for source in range(chips):
-                    pass_on(job, source, core).wait_send()
-                    pass_on(job, source, 1 - core).wait_recv()
-        for n_short in sorted({jobs[job][5] for job in mine}):
-            @pl.when(functools.reduce(jnp.logical_or, [chip == jobs[job][2] for job in mine if jobs[job][5] == n_short]))
-            def _():
-                n_pad = padded(n_short)
-                square = pl.ds(0, n_pad)
-                step = functools.partial(ns_step, n_short, core, partner, remote, x_ref.at[turn, :, pl.ds(0, n_pad)],
-                                         a_ref.at[square, square], b_ref.at[square, square], tile_send, tile_recv)
-                lax.fori_loop(0, NS_STEPS, step, 0)
-        for job in mine:
-            owner = jobs[job][2]
-
-            @pl.when(chip == owner)
-            def _():
-                for target in range(chips):
-                    (hand_out_own(job) if target == owner else hand_out(job, target)).start()
+                    start = turn * turn_rows + slot * n_pad
+                    x_ref[start + n_short:start + n_pad, :] = jnp.zeros((n_pad - n_short, n_long), jnp.bfloat16)
+
+    def receive(job):
+        collect_own(job).wait()
+        pass_on(job, jobs[job][2], core).start()
+        for source in range(chips):
+            if source != jobs[job][2]:
+                collect(job, source).wait_recv()
+                pass_on(job, source, core).start()
+        for source in range(chips):
+            pass_on(job, source, core).wait_send()
+            pass_on(job, source, 1 - core).wait_recv()
+
+    def give_back(job):
+        if keep:
+            store(job).start()
+            return
+        for target in range(chips):
+            (hand_out_own(job) if target == jobs[job][2] else hand_out(job, target)).start()
+
+    for n_short in sorted({job[5] for job in jobs}):
+        mine = [job for job in range(len(jobs)) if jobs[job][5] == n_short]
+
+        def work(turn, carry):
+            def each(body):
+                for job in mine:
+                    pl.when(jnp.logical_and(chip == jobs[job][2], turn == jobs[job][3]))(functools.partial(body, job))
+
+            each(receive)
+            each_late(late_begin)
+            newton_schulz(padded(n_short) // 2, core, partner, remote, x_ref, turn * turn_rows, a_ref, b_ref, far_ref, tile_send, tile_recv)
+            each(give_back)
+            each_late(late_middle)
+            return carry
+
+        @pl.when(functools.reduce(jnp.logical_or, [chip == jobs[job][2] for job in mine]))
+        def _():
+            lax.fori_loop(0, 1 + max(jobs[job][3] for job in mine), work, 0)
 
     for job, (_, _, owner, _, _, _) in enumerate(jobs):
         @pl.when(chip == owner)
         def _():
+            if keep:
+                store(job).wait()
+                return
             hand_out_own(job).wait()
             for target in range(chips):
                 if target != owner:
@@ -165,106 +224,125 @@
         @pl.when(chip != owner)
         def _():
             collect(job, chip).wait_send()
-            hand_out(job, chip).wait_recv()
+            if not keep:
+                hand_out(job, chip).wait_recv()
+    each_late(late_end, lambda index: late_hand_out(index, chip).wait_recv())
 
 
 def padded(n_short):
     return -(-n_short // TILE) * TILE
 
 
+def rows_of_turn(jobs, turn):
+    return 2 * padded(max([job[5] for job in jobs if job[3] == turn], default=0))
+
+
 TILE = 512
 
 
-def ns_step(n_short, core, partner, remote, x_ref, a_ref, b_ref, tile_send, tile_recv, step, carry):
-    n_pad, n_long = x_ref.shape[1:]
-    x_now, x_next = x_ref.at[step % 2], x_ref.at[(step + 1) % 2]
-    tiles = n_pad // TILE
-
-    def span(i, length=TILE):
-        return pl.ds(pl.multiple_of(i * length, length), length)
-
-    def send(stage, ref):
-        remote(ref, ref, tile_send.at[stage], tile_recv.at[stage], partner).start()
-
-    def await_tiles(stage, sent, received):
-        def view(count):
-            return x_ref.at[0, pl.ds(0, count * TILE * TILE // n_long), :]
-        for side in range(2):
-            @pl.when(core == side)
-            def _():
-                remote(view(sent[side]), view(sent[side]), tile_send.at[stage], tile_recv.at[stage], partner).wait_send()
-                remote(view(received[side]), view(received[side]), tile_send.at[stage], tile_recv.at[stage], partner).wait_recv()
-
-    def owner_of(i, j):
-        return (i // 2 + j) % 2
-
-    def upper(stage, ref, body):
-        def visit(t, c):
-            i, j = t // tiles, t % tiles
-
-            @pl.when(jnp.logical_and(i <= j, owner_of(i, j) == core))
-            def _():
-                tile = body(i, j)
-                ref[span(i), span(j)] = tile
-                send(stage, ref.at[span(i), span(j)])
-
-                @pl.when(i != j)
-                def _():
-                    ref[span(j), span(i)] = tile.T
-                    send(stage, ref.at[span(j), span(i)])
+def newton_schulz(half, core, partner, remote, x_ref, base, a_ref, b_ref, far_ref, tile_send, tile_recv):
+    n_long = x_ref.shape[1]
+    near, far = (pl.ds(pl.multiple_of(side * half, half), half) for side in (core, 1 - core))
+    mine = pl.ds(0, half)
+
+    def rows(slot, side):
+        return pl.ds(pl.multiple_of(base + (2 * slot + side) * half, 256), half)
+
+    def a_copy(parity):
+        return remote(a_ref.at[mine, near], far_ref.at[parity, mine, mine], tile_send.at[parity], tile_recv.at[parity], partner)
+
+    def x_copy(slot, columns):
+        there = x_ref.at[rows(slot, core), columns]
+        return remote(there, there, tile_send.at[2 + slot], tile_recv.at[2 + slot], partner)
+
+    def dot(left, right):
+        return jnp.dot(left, right, preferred_element_type=jnp.float32)
+
+    def dot_t(left, right):
+        return lax.dot_general(left, right, (((1,), (1,)), ((), ())), preferred_element_type=jnp.float32)
+
+    def piece(index):
+        return pl.ds(pl.multiple_of(index * (half // 2), half // 2), half // 2)
+
+    def poly(columns, square):
+        def visit(index, c):
+            band = piece(index)
+            tile = COEF_B * a_ref[band, columns].astype(jnp.float32)
+            tile += COEF_C * square(band).astype(jnp.bfloat16).astype(jnp.float32)
+            b_ref[band, columns] = tile.astype(jnp.bfloat16)
             return c
-        lax.fori_loop(0, tiles * tiles, visit, 0)
-        count = [sum(1 + (i != j) for i in range(tiles) for j in range(i, tiles) if owner_of(i, j) == side) for side in range(2)]
-        await_tiles(stage, count, count[::-1])
-
-    def gram(i, j):
-        tile = lax.dot_general(x_now[span(i), :], x_now[span(j), :], (((1,), (1,)), ((), ())), preferred_element_type=jnp.float32)
-        return tile.astype(jnp.bfloat16)
-
-    def poly(i, j):
-        square = jnp.dot(a_ref[span(i), :n_short], a_ref[:n_short, span(j)], preferred_element_type=jnp.float32)
-        tile = COEF_B * a_ref[span(i), span(j)].astype(jnp.float32) + COEF_C * square.astype(jnp.bfloat16).astype(jnp.float32)
-        return tile.astype(jnp.bfloat16)
-
-    upper(0, a_ref, gram)
-    upper(1, b_ref, poly)
-    height = n_short // 2
-    wide = n_long // TILE // 2
-
-    def apply(t, c):
-        rows, cols = span(t // wide, height), span(core * wide + t % wide)
-        update = jnp.dot(b_ref[rows, :n_short], x_now[:n_short, cols], preferred_element_type=jnp.float32).astype(jnp.bfloat16)
-        x_next[rows, cols] = (COEF_A * x_now[rows, cols].astype(jnp.float32) + update.astype(jnp.float32)).astype(jnp.bfloat16)
-        send(2, x_next.at[rows, cols])
-        return c
-
-    lax.fori_loop(0, 2 * wide, apply, 0)
-    half = x_ref.at[0, pl.ds(0, n_short // 2), :]
-    remote(half, half, tile_send.at[2], tile_recv.at[2], partner).wait()
-    return carry
-
-
-def orthogonalize(jobs, stacks, collective_id):
-    shorts = [rows.shape[1] * (GROUP if axis == 0 else 1) for rows, axis in stacks]
-    n_long = stacks[0][0].shape[2] * (GROUP if stacks[0][1] == 1 else 1)
-    full = [(stack, k, chip, turn, stacks[stack][1], shorts[stack]) for stack, k, chip, turn in jobs]
-    n_pad = padded(max(shorts))
-    turns = 1 + max(job[3] for job in jobs)
+        lax.fori_loop(0, 2, visit, 0)
+
+    def step(count, carry):
+        now, later = count % 2, (count + 1) % 2
+
+        def gram(turn, c):
+            side = core + (turn // 2) * (1 - 2 * core)
+            band, columns = piece(turn % 2), pl.ds(pl.multiple_of(side * half, half), half)
+            left = x_ref[pl.ds(pl.multiple_of(base + (2 * now + core) * half + (turn % 2) * (half // 2), 128), half // 2), :]
+            a_ref[band, columns] = dot_t(left, x_ref[rows(now, side), :]).astype(jnp.bfloat16)
+            pl.when(turn == 1)(lambda: a_copy(now).start())
+            pl.when(jnp.logical_and(turn == 1, count > 0))(lambda: x_copy(now, pl.ds(0, n_long)).wait())
+            return c
+
+        lax.fori_loop(0, 4, gram, 0)
+        poly(near, lambda band: dot(a_ref[band, near], a_ref[mine, near]) + dot_t(a_ref[band, far], a_ref[mine, far]))
+        a_copy(now).wait()
+        poly(far, lambda band: dot(a_ref[band, near], a_ref[mine, far]) + dot(a_ref[band, far], far_ref[now, mine, mine]))
+
+        def apply(t, c):
+            columns = pl.ds(pl.multiple_of(t * TILE, TILE), TILE)
+            both = pl.ds(pl.multiple_of(base + 2 * now * half, 256), 2 * half)
+            update = dot(b_ref[mine, pl.ds(0, 2 * half)], x_ref[both, columns]).astype(jnp.bfloat16)
+            old = x_ref[rows(now, core), columns].astype(jnp.float32)
+            x_ref[rows(later, core), columns] = (COEF_A * old + update.astype(jnp.float32)).astype(jnp.bfloat16)
+            x_copy(later, columns).start()
+            return c
+
+        lax.fori_loop(0, n_long // TILE, apply, 0)
+        return carry
+
+    lax.fori_loop(0, NS_STEPS, step, 0)
+    x_copy(NS_STEPS % 2, pl.ds(0, n_long)).wait()
+
+
+def orthogonalize(jobs, stacks, collective_id, keep=False, late=None):
+    def whole(shapes, axes, given):
+        shorts = [shape[1] * (GROUP if axis == 0 else 1) for shape, axis in zip(shapes, axes)]
+        return [(stack, k, chip, turn, axes[stack], shorts[stack]) for stack, k, chip, turn in given]
+
+    shapes, axes = [rows.shape for rows, _ in stacks], [axis for _, axis in stacks]
+    full = whole(shapes, axes, jobs)
+    n_long = shapes[0][2] * (GROUP if axes[0] == 1 else 1)
+    n_pad = padded(max(job[5] for job in full))
+    x_rows = sum(rows_of_turn(full, turn) for turn in range(2))
     n_jobs, chips = len(jobs), GROUP // 2
-    dma = pltpu.SemaphoreType.DMA
+    dma, bf16 = pltpu.SemaphoreType.DMA, jnp.bfloat16
+    args = [rows for rows, _ in stacks]
+    kept_rows = max((job[3] + 1) * job[5] for job in full)
+    out_shape = [jax.ShapeDtypeStruct((kept_rows, n_long), bf16)] if keep else [jax.ShapeDtypeStruct(shape, bf16) for shape in shapes]
+    scratch = [pltpu.VMEM((x_rows, n_long), bf16), pltpu.VMEM((n_pad // 2, n_pad), bf16),
+               pltpu.VMEM((n_pad // 2, n_pad), bf16), pltpu.VMEM((2, n_pad // 2, n_pad // 2), bf16),
+               dma((n_jobs,)), dma((n_jobs, chips)), dma((n_jobs, chips)), dma((n_jobs, chips)), dma((n_jobs, chips)),
+               dma((n_jobs,)), dma((n_jobs,)), dma((4,)), dma((4,))]
+    full_late = []
+    if late is not None:
+        late_jobs, late_shapes, late_axes, kept = late
+        full_late = whole(late_shapes, late_axes, late_jobs)
+        args.append(kept)
+        out_shape += [jax.ShapeDtypeStruct(shape, bf16) for shape in late_shapes]
+        scratch += [dma((len(late_jobs), chips)), dma((len(late_jobs),)), dma((len(late_jobs), 2))]
+        scratch += [pltpu.VMEM((2,) + tuple(shape[1:]), bf16) for shape in late_shapes]
     return pl.pallas_call(
-        functools.partial(ortho_kernel, full),
-        out_shape=[jax.ShapeDtypeStruct(rows.shape, rows.dtype) for rows, _ in stacks],
-        in_specs=[pl.BlockSpec(memory_space=pl.ANY)] * len(stacks),
-        out_specs=[pl.BlockSpec(memory_space=pl.ANY)] * len(stacks),
-        scratch_shapes=[pltpu.VMEM((turns, 2, n_pad, n_long), jnp.bfloat16), pltpu.VMEM((n_pad, n_pad), jnp.bfloat16),
-                        pltpu.VMEM((n_pad, n_pad), jnp.bfloat16),
-                        dma((n_jobs,)), dma((n_jobs, chips)), dma((n_jobs, chips)), dma((n_jobs, chips)), dma((n_jobs, chips)),
-                        dma((n_jobs,)), dma((n_jobs,)), dma((3,)), dma((3,))],
+        functools.partial(ortho_kernel, full, full_late, keep),
+        out_shape=out_shape,
+        in_specs=[pl.BlockSpec(memory_space=pl.ANY)] * len(args),
+        out_specs=[pl.BlockSpec(memory_space=pl.ANY)] * len(out_shape),
+        scratch_shapes=scratch,
         compiler_params=pltpu.CompilerParams(collective_id=collective_id, has_side_effects=True, vmem_limit_bytes=58 << 20),
         cost_estimate=pl.CostEstimate(flops=2_000_000_000, bytes_accessed=16 << 20, transcendentals=0),
         name=f'ortho{collective_id}',
-    )(*[rows for rows, _ in stacks])
+    )(*args)
 
 
 SLOTS = 5
@@ -378,9 +456,46 @@
     return mom_new, jnp.sum(mom_new * mom_new, axis=(1, 2))
 
 
-def to_send(mom_new, norm_sq, transposed):
-    x_rows = (mom_new / (jnp.sqrt(norm_sq)[:, None, None] + EPSILON)).astype(jnp.bfloat16)
-    return jnp.swapaxes(x_rows, 1, 2) if transposed else x_rows
+def to_send(mom_new, norm_sq):
+    return (mom_new / (jnp.sqrt(norm_sq)[:, None, None] + EPSILON)).astype(jnp.bfloat16)
+
+
+def turned_kernel(norm_ref, mom_ref, out_ref):
+    out_ref[0] = (mom_ref[0] / norm_ref[pl.program_id(0)]).astype(jnp.bfloat16).T
+
+
+def to_send_turned(mom_new, norm_sq):
+    count, rows, cols = mom_new.shape
+    wide = cols
+    return pl.pallas_call(
+        turned_kernel,
+        grid=(count, cols // wide),
+        out_shape=jax.ShapeDtypeStruct((count, cols, rows), jnp.bfloat16),
+        in_specs=[pl.BlockSpec(memory_space=pltpu.SMEM), pl.BlockSpec((1, rows, wide), lambda k, j: (k, 0, j))],
+        out_specs=pl.BlockSpec((1, wide, rows), lambda k, j: (k, j, 0)),
+        name='to_send_turned',
+    )(jnp.sqrt(norm_sq) + EPSILON, mom_new)
+
+
+def weights_kernel(scale, ortho_ref, master_ref, new_ref, short_ref):
+    ortho = ortho_ref[0].T.astype(jnp.float32)
+    new = master_ref[0] - LEARN_RATE * (scale * ortho + WEIGHT_DECAY * master_ref[0])
+    new_ref[0] = new
+    short_ref[0] = new.astype(jnp.bfloat16)
+
+
+def new_weights_turned(ortho_turned, master_old, n_rows, n_cols):
+    count, rows, cols = master_old.shape
+    wide = cols
+    straight = pl.BlockSpec((1, rows, wide), lambda k, j: (k, 0, j))
+    return pl.pallas_call(
+        functools.partial(weights_kernel, 0.2 * math.sqrt(max(n_rows, n_cols))),
+        grid=(count, cols // wide),
+        out_shape=[jax.ShapeDtypeStruct(master_old.shape, jnp.float32), jax.ShapeDtypeStruct(master_old.shape, jnp.bfloat16)],
+        in_specs=[pl.BlockSpec((1, wide, rows), lambda k, j: (k, j, 0)), straight],
+        out_specs=[straight, straight],
+        name='new_weights_turned',
+    )(ortho_turned, master_old)
 
 
 def new_weights(ortho_rows, master_old, n_rows, n_cols):
@@ -404,18 +519,17 @@
 
         mn_attn, part_attn = momentum(r_attn, m_attn)
         mn_up, part_up = momentum(r_up, m_up)
-        mn_up = with_layout_constraint(mn_up, Layout((0, 1, 2)))
         parts = sum_over_data(jnp.concatenate([part_attn, part_up]), 0)
-        x_attn = to_send(mn_attn, parts[:2], False)
-        x_up = to_send(mn_up, parts[2:], True)
-        or_attn, or_up = orthogonalize(FIRST_JOBS, [(x_attn, 0), (x_up, 1)], 1)
+        x_attn = to_send(mn_attn, parts[:2])
+        x_up = to_send_turned(mn_up, parts[2:])
+        kept, = orthogonalize(FIRST_JOBS, [(x_attn, 0), (x_up, 1)], 1, keep=True)
+
+        r_down, kept = lax.optimization_barrier((r_down, kept))
+        mn_down, part_down = momentum(r_down, m_down)
+        x_down = to_send(mn_down, sum_over_data(part_down, 4))
+        or_down, or_attn, or_up = orthogonalize(LAST_JOBS, [(x_down, 0)], 5, late=(FIRST_JOBS, (x_attn.shape, x_up.shape), (0, 1), kept))
         wn_attn, wb_attn = new_weights(or_attn, w_attn, 2048, 2048)
-        wn_up, wb_up = new_weights(jnp.swapaxes(or_up, 1, 2), w_up, 2048, 1408)
-
-        r_down, wn_attn, wb_attn, wn_up, wb_up = lax.optimization_barrier((r_down, wn_attn, wb_attn, wn_up, wb_up))
-        mn_down, part_down = momentum(r_down, m_down)
-        x_down = to_send(mn_down, sum_over_data(part_down, 4), False)
-        or_down, = orthogonalize(LAST_JOBS, [(x_down, 0)], 5)
+        wn_up, wb_up = new_weights_turned(or_up, w_up, 2048, 1408)
         wn_down, wb_down = new_weights(or_down, w_down, 1408, 2048)
         return (mn_attn, wn_attn, wb_attn, mn_up, wn_up, wb_up, mn_down, wn_down, wb_down)
 

time: 928 us -> 831 us (0.90)
  Pallas kernels: 831 us -> 723 us
  waiting for transfers between devices: 1.4 us -> 44 us
  local copies, waits for them, and re-layouts: 28 us -> 6.67 us
  other arithmetic: 52.5 us -> 42.8 us
    pallas_call x2 -> x4, Pallas kernels: 487 us -> 389 us  [the longest x2 376 us: orthogonalize(): pl.pallas_call(functools.partial(ortho_kernel, full, full_late, keep), ou...]
    reduce_scatter x2, waiting for transfers between devices: 0.02 us -> 42.6 us  [reduce_rows(): return lax.psum_scatter(grad[0], 'data', scatter_dimension=1, tiled=True)]
    unnamed x15 -> x10, local copies, waits for them, and re-layouts: 17.7 us -> 2.54 us
  transfers between devices with their start and end apart: 2 -> 2, of which waited for: 0 -> 2; matrix products, arithmetic and copies ran while one was open for 5% -> 2% of each run, Pallas kernels for 70% -> 67%
where the time goes in v2:
time: 831 us; the launch traced here: 830 us
  Pallas kernels  723 us (87%)
  waiting for transfers between devices  44 us (5%)
  other arithmetic  42.8 us (5%)
  between operations  14.1 us (2%)
    pallas_call x2, Pallas kernels, orthogonalize(): pl.pallas_call(functools.partial(ortho_kernel, full, full_late, keep), ou...  376 us
    pallas_call x1, Pallas kernels, reduce_rows_kernel(): pl.pallas_call(functools.partial(reduce_kernel, count * per_matrix, per_m...  322 us
    reduce_scatter x2, waiting for transfers between devices, reduce_rows(): return lax.psum_scatter(grad[0], 'data', scatter_dimension=1, tiled=True)  42.6 us
    reduce_sum x3, other arithmetic, momentum(): return (mom_new, jnp.sum(mom_new * mom_new, axis=(1, 2)))  21.3 us
  transfers between devices with their start and end apart: 2, of which 2 were waited for; matrix products, arithmetic and copies ran while one was open for 2% of the time, Pallas kernels for 67%

profile of v2, /device:TPU:0, one launch (start us, length us, event | category | flops | bytes accessed | tf_op | source)
XLA Modules:
  0.0 830.4 jit_solution(12451734107766521285)
XLA Ops:
  7.2 0.7 reduce-scatter.3.cloned.1.call-update
  8.0 0.7 reduce-scatter.5.cloned.1.call-update
  8.7 322.0 %reduce7.1 = f32[4,256,1408]{2,1,0:T(8,128)S(1)} custom-call(f32[4,2,2,2,256,1408]{5,4,3,2,1,0:T(8,128)} %bitcast.3), custom_call_target="tpu_custom_call" | custom-call | flops 1000000000 | bytes 67108864 | tf_op jit(solution)/shard_map/reduce7/pallas_call | solution.py:439
  330.7 2.5 copy-done
  333.3 5.1 reduce-scatter.3.cloned.1.call-done
  338.3 6.8 multiply_reduce_fusion.2
  345.1 6.2 multiply_reduce_fusion.1
  351.4 0.7 broadcast_in_dim.13.part_ref
  352.1 6.0 share0.1
  358.1 0.8 slice_reduce_fusion.1
  359.6 0.6 sqrt_add_fusion.1.norm_ref
  360.2 5.1 to_send_turned.1.refs_1_
  365.3 4.0 divide_convert_fusion.1.refs_0_
  369.4 220.2 %ortho1.1.refs_1_ = bf16[2816,2048]{1,0:T(8,128)(2,1)} custom-call(bf16[2,256,2048]{2,1,0:T(8,128)(2,1)} %divide_convert_fusion.1.refs_0_, bf16[4,1408,256]{2,1,0:T(8,128)(2,1)} %to_send_turned.1.refs_1_), custom_call_target="tpu_custom_call" | custom-call | flops 2000000000 | bytes 16777216 | tf_op jit(solution)/shard_map/ortho1/pallas_call | solution.py:336
  589.6 37.6 %reduce-scatter.5.cloned.1.call-done = f32[4,176,2048]{2,1,0:T(8,128)} async-done(((f32[4,1408,2048]{2,1,0:T(8,128)}), f32[4,176,2048]{2,1,0:T(8,128)}) %reduce-scatter.5.cloned.1.call-update) | async-done | bytes 5767184 | tf_op jit(solution)/shard_map/reduce_scatter | solution.py:513
  627.2 8.3 multiply_reduce_fusion
  635.4 0.7 broadcast_in_dim.14.part_ref
  636.1 6.1 share4.1
  642.2 0.8 slice_reduce_fusion
  643.7 5.0 divide_convert_fusion.refs_0_
  648.7 155.4 %ortho5.1 = (bf16[4,176,2048]{2,1,0:T(8,128)(2,1)}, bf16[2,256,2048]{2,1,0:T(8,128)(2,1)}, bf16[4,1408,256]{2,1,0:T(8,128)(2,1)}) custom-call(bf16[4,176,2048]{2,1,0:T(8,128)(2,1)} %divide_convert_fusion.refs_0_, bf16[2816,2048]{1,0:T(8,128)(2,1)} %ortho1.1.refs_1_), custom_call_target="tpu_custom_call" | custom-call | flops 2000000000 | bytes 16777216 | tf_op jit(solution)/shard_map/ortho5/pallas_call | solution.py:336
  804.1 7.8 new_weights_turned.1
  811.9 7.8 fusion.2
  819.7 3.8 fusion.3
  (22 shorter events, 1.5 us)
Async XLA Ops:
  7.2 331.2 %reduce-scatter.3.cloned.1.call-start = ((), (), s32[]{:S(2)}) async-start(), calls=%async_computation.2 | async-start | bytes 37748736 | tf_op jit(solution)/shard_map/reduce_scatter | solution.py:513
  7.9 619.2 %reduce-scatter.5.cloned.1.call-start = ((), (), s32[]{:S(2)}) async-start(), calls=%async_computation.3 | async-start | bytes 51904512 | tf_op jit(solution)/shard_map/reduce_scatter | solution.py:513
  330.7 2.5 copy-start
  338.3 6.8 copy-start.1
  804.1 7.8 copy-start.3
  811.9 7.8 copy-start.2
  811.9 7.8 copy-start.4
Sparse Core Ops, SparseCore 0:
  11.5 326.8 reduce-scatter.2
  341.9 285.2 reduce-scatter.4

commit v3 on v2

--- a/solution.py
+++ b/solution.py
@@ -65,10 +65,35 @@
     return ref.at[pl.ds(start, size), :] if axis == 0 else ref.at[:, pl.ds(start, size)]
 
 
-def ortho_kernel(jobs, late, keep, *refs):
+def normalize(me, mom_ref, part_ref, all_ref, wide_ref, x_ref, send_sem, recv_sem, load_sem):
+    def share(source, target):
+        return pltpu.make_async_remote_copy(
+            src_ref=part_ref, dst_ref=all_ref.at[source], send_sem=send_sem.at[target], recv_sem=recv_sem.at[source],
+            device_id={'data': target}, device_id_type=pl.DeviceIdType.MESH)
+
+    others = [lax.rem(me + step, GROUP) for step in range(1, GROUP)]
+    for other in others:
+        share(me, other).start()
+    load = pltpu.make_async_copy(mom_ref, wide_ref, load_sem)
+    load.start()
+    all_ref[me] = part_ref[...]
+    for other in others:
+        share(me, other).wait_send()
+        share(other, other).wait_recv()
+    total = all_ref[0]
+    for device in range(1, GROUP):
+        total += all_ref[device]
+    norm = jnp.sqrt(total) + EPSILON
+    load.wait()
+    for k in range(mom_ref.shape[0]):
+        x_ref[k] = (wide_ref[k] / norm[k:k + 1, :1]).astype(jnp.bfloat16)
+    return x_ref
+
+
+def ortho_kernel(jobs, late, keep, raw, *refs):
     n_stacks = 1 + max(job[0] for job in jobs)
     n_late = 1 + max([job[0] for job in late], default=-1)
-    n_in = n_stacks + (n_late > 0)
+    n_in = n_stacks + raw + (n_late > 0)
     n_out = 1 if keep else n_stacks
     ins, kept_in = refs[:n_stacks], refs[n_in - 1]
     outs, late_outs = refs[n_in:n_in + n_out], refs[n_in + n_out:n_in + n_out + n_late]
@@ -79,6 +104,8 @@
     chip, core = me // 2, me % 2
     partner = me + 1 - 2 * core
     greet_all(me)
+    if raw:
+        ins = (normalize(me, ins[0], refs[n_stacks], *scratch[-6:]),)
     n_long = x_ref.shape[1]
     chips = GROUP // 2
     turn_rows = rows_of_turn(jobs, 0)
@@ -184,12 +211,14 @@
             pass_on(job, source, core).wait_send()
             pass_on(job, source, 1 - core).wait_recv()
 
-    def give_back(job):
-        if keep:
-            store(job).start()
-            return
+    def give_back(t, job):
+        columns = pl.ds(pl.multiple_of(t * TILE, TILE), TILE)
         for target in range(chips):
-            (hand_out_own(job) if target == jobs[job][2] else hand_out(job, target)).start()
+            here, there = block(job, last, 2 * target + core).at[:, columns], rows_out(job).at[:, columns]
+            if target == jobs[job][2]:
+                pltpu.make_async_copy(here, there, own_sem.at[job]).start()
+            else:
+                remote(here, there, back_sem.at[job, target], got_sem.at[job], 2 * target + core).start()
 
     for n_short in sorted({job[5] for job in jobs}):
         mine = [job for job in range(len(jobs)) if jobs[job][5] == n_short]
@@ -201,8 +230,10 @@
 
             each(receive)
             each_late(late_begin)
-            newton_schulz(padded(n_short) // 2, core, partner, remote, x_ref, turn * turn_rows, a_ref, b_ref, far_ref, tile_send, tile_recv)
-            each(give_back)
+            newton_schulz(padded(n_short) // 2, core, partner, remote, x_ref, turn * turn_rows, a_ref, b_ref, far_ref, tile_send, tile_recv,
+                          None if keep else lambda t: each(functools.partial(give_back, t)))
+            if keep:
+                each(lambda job: store(job).start())
             each_late(late_middle)
             return carry
 
@@ -240,7 +271,7 @@
 TILE = 512
 
 
-def newton_schulz(half, core, partner, remote, x_ref, base, a_ref, b_ref, far_ref, tile_send, tile_recv):
+def newton_schulz(half, core, partner, remote, x_ref, base, a_ref, b_ref, far_ref, tile_send, tile_recv, finish=None):
     n_long = x_ref.shape[1]
     near, far = (pl.ds(pl.multiple_of(side * half, half), half) for side in (core, 1 - core))
     mine = pl.ds(0, half)
@@ -254,6 +285,14 @@
     def x_copy(slot, columns):
         there = x_ref.at[rows(slot, core), columns]
         return remote(there, there, tile_send.at[2 + slot], tile_recv.at[2 + slot], partner)
+
+    def end_copy(t):
+        there = x_ref.at[rows(NS_STEPS % 2, core), pl.ds(pl.multiple_of(t * TILE, TILE), TILE)]
+        return remote(there, there, tile_send.at[4 + t], tile_recv.at[4 + t], partner)
+
+    def end(t):
+        end_copy(t).wait()
+        finish(t)
 
     def dot(left, right):
         return jnp.dot(left, right, preferred_element_type=jnp.float32)
@@ -296,17 +335,26 @@
             update = dot(b_ref[mine, pl.ds(0, 2 * half)], x_ref[both, columns]).astype(jnp.bfloat16)
             old = x_ref[rows(now, core), columns].astype(jnp.float32)
             x_ref[rows(later, core), columns] = (COEF_A * old + update.astype(jnp.float32)).astype(jnp.bfloat16)
-            x_copy(later, columns).start()
+            if finish is None:
+                x_copy(later, columns).start()
+                return c
+            is_last = count == NS_STEPS - 1
+            pl.when(jnp.logical_not(is_last))(lambda: x_copy(later, columns).start())
+            pl.when(is_last)(lambda: end_copy(t).start())
+            pl.when(jnp.logical_and(is_last, t > 0))(lambda: end(t - 1))
             return c
 
         lax.fori_loop(0, n_long // TILE, apply, 0)
         return carry
 
     lax.fori_loop(0, NS_STEPS, step, 0)
-    x_copy(NS_STEPS % 2, pl.ds(0, n_long)).wait()
-
-
-def orthogonalize(jobs, stacks, collective_id, keep=False, late=None):
+    if finish is None:
+        x_copy(NS_STEPS % 2, pl.ds(0, n_long)).wait()
+    else:
+        end(n_long // TILE - 1)
+
+
+def orthogonalize(jobs, stacks, collective_id, keep=False, late=None, part=None):
     def whole(shapes, axes, given):
         shorts = [shape[1] * (GROUP if axis == 0 else 1) for shape, axis in zip(shapes, axes)]
         return [(stack, k, chip, turn, axes[stack], shorts[stack]) for stack, k, chip, turn in given]
@@ -319,12 +367,14 @@
     n_jobs, chips = len(jobs), GROUP // 2
     dma, bf16 = pltpu.SemaphoreType.DMA, jnp.bfloat16
     args = [rows for rows, _ in stacks]
+    if part is not None:
+        args.append(jnp.broadcast_to(jnp.pad(part, (0, 8 - part.shape[0]))[:, None], (8, 128)))
     kept_rows = max((job[3] + 1) * job[5] for job in full)
     out_shape = [jax.ShapeDtypeStruct((kept_rows, n_long), bf16)] if keep else [jax.ShapeDtypeStruct(shape, bf16) for shape in shapes]
     scratch = [pltpu.VMEM((x_rows, n_long), bf16), pltpu.VMEM((n_pad // 2, n_pad), bf16),
                pltpu.VMEM((n_pad // 2, n_pad), bf16), pltpu.VMEM((2, n_pad // 2, n_pad // 2), bf16),
                dma((n_jobs,)), dma((n_jobs, chips)), dma((n_jobs, chips)), dma((n_jobs, chips)), dma((n_jobs, chips)),
-               dma((n_jobs,)), dma((n_jobs,)), dma((4,)), dma((4,))]
+               dma((n_jobs,)), dma((n_jobs,)), dma((4 + n_long // TILE,)), dma((4 + n_long // TILE,))]
     full_late = []
     if late is not None:
         late_jobs, late_shapes, late_axes, kept = late
@@ -333,10 +383,15 @@
         out_shape += [jax.ShapeDtypeStruct(shape, bf16) for shape in late_shapes]
         scratch += [dma((len(late_jobs), chips)), dma((len(late_jobs),)), dma((len(late_jobs), 2))]
         scratch += [pltpu.VMEM((2,) + tuple(shape[1:]), bf16) for shape in late_shapes]
+    specs = [pl.BlockSpec(memory_space=pl.ANY)] * len(args)
+    if part is not None:
+        specs[len(stacks)] = pl.BlockSpec(memory_space=pltpu.VMEM)
+        scratch += [pltpu.VMEM((GROUP, 8, 128), jnp.float32), pltpu.VMEM(shapes[0], jnp.float32), pltpu.VMEM(shapes[0], bf16),
+                    dma((GROUP,)), dma((GROUP,)), dma]
     return pl.pallas_call(
-        functools.partial(ortho_kernel, full, full_late, keep),
+        functools.partial(ortho_kernel, full, full_late, keep, part is not None),
         out_shape=out_shape,
-        in_specs=[pl.BlockSpec(memory_space=pl.ANY)] * len(args),
+        in_specs=specs,
         out_specs=[pl.BlockSpec(memory_space=pl.ANY)] * len(out_shape),
         scratch_shapes=scratch,
         compiler_params=pltpu.CompilerParams(collective_id=collective_id, has_side_effects=True, vmem_limit_bytes=58 << 20),
@@ -526,8 +581,8 @@
 
         r_down, kept = lax.optimization_barrier((r_down, kept))
         mn_down, part_down = momentum(r_down, m_down)
-        x_down = to_send(mn_down, sum_over_data(part_down, 4))
-        or_down, or_attn, or_up = orthogonalize(LAST_JOBS, [(x_down, 0)], 5, late=(FIRST_JOBS, (x_attn.shape, x_up.shape), (0, 1), kept))
+        or_down, or_attn, or_up = orthogonalize(
+            LAST_JOBS, [(mn_down, 0)], 5, late=(FIRST_JOBS, (x_attn.shape, x_up.shape), (0, 1), kept), part=part_down)
         wn_attn, wb_attn = new_weights(or_attn, w_attn, 2048, 2048)
         wn_up, wb_up = new_weights_turned(or_up, w_up, 2048, 1408)
         wn_down, wb_down = new_weights(or_down, w_down, 1408, 2048)

time: 831 us -> 819 us (0.986)
  transfers between devices with their start and end apart: 2 -> 2, of which waited for: 2 -> 2; matrix products, arithmetic and copies ran while one was open for 2% -> 2% of each run, Pallas kernels for 67% -> 68%
where the time goes in v3:
time: 819 us
  Pallas kernels  718 us (88%)
  waiting for transfers between devices  43.9 us (5%)
  other arithmetic  37.7 us (5%)
  between operations  14.1 us (2%)
    pallas_call x2, Pallas kernels, orthogonalize(): pl.pallas_call(functools.partial(ortho_kernel, full, full_late, keep, par...  377 us
    pallas_call x1, Pallas kernels, reduce_rows_kernel(): pl.pallas_call(functools.partial(reduce_kernel, count * per_matrix, per_m...  322 us
    reduce_scatter x2, waiting for transfers between devices, reduce_rows(): return lax.psum_scatter(grad[0], 'data', scatter_dimension=1, tiled=True)  42.6 us
    reduce_sum x3, other arithmetic, momentum(): return (mom_new, jnp.sum(mom_new * mom_new, axis=(1, 2)))  21.3 us
  transfers between devices with their start and end apart: 2, of which 2 were waited for; matrix products, arithmetic and copies ran while one was open for 2% of the time, Pallas kernels for 68%

profile of v3, /device:TPU:0, one launch (start us, length us, event | category | flops | bytes accessed | tf_op | source)
XLA Modules:
  0.0 818.7 jit_solution(10987069891975259873)
XLA Ops:
  7.2 0.7 reduce-scatter.3.cloned.1.call-update
  8.0 0.7 reduce-scatter.5.cloned.1.call-update
  8.7 322.0 %reduce7.1 = f32[4,256,1408]{2,1,0:T(8,128)S(1)} custom-call(f32[4,2,2,2,256,1408]{5,4,3,2,1,0:T(8,128)} %bitcast.5), custom_call_target="tpu_custom_call" | custom-call | flops 1000000000 | bytes 67108864 | tf_op jit(solution)/shard_map/reduce7/pallas_call | solution.py:494
  330.7 2.5 copy-done
  333.3 5.1 reduce-scatter.3.cloned.1.call-done
  338.3 6.8 multiply_reduce_fusion.2
  345.1 6.2 multiply_reduce_fusion.1
  351.3 0.1 fusion
  351.4 0.7 broadcast_in_dim.24.part_ref
  352.1 6.0 share0.1
  358.1 0.8 slice_reduce_fusion
  358.9 0.6 gather_fusion
  359.5 0.1 select_reduce_fusion
  359.6 0.6 sqrt_add_fusion.norm_ref
  360.2 5.1 to_send_turned.1.refs_1_
  365.3 4.0 divide_convert_fusion.refs_0_
  369.4 220.3 %ortho1.1.refs_2_ = bf16[2816,2048]{1,0:T(8,128)(2,1)} custom-call(bf16[2,256,2048]{2,1,0:T(8,128)(2,1)} %divide_convert_fusion.refs_0_, bf16[4,1408,256]{2,1,0:T(8,128)(2,1)} %to_send_turned.1.refs_1_), custom_call_target="tpu_custom_call" | custom-call | flops 2000000000 | bytes 16777216 | tf_op jit(solution)/shard_map/ortho1/pallas_call | solution.py:391
  589.7 37.5 %reduce-scatter.5.cloned.1.call-done = f32[4,176,2048]{2,1,0:T(8,128)} async-done(((f32[4,1408,2048]{2,1,0:T(8,128)}), f32[4,176,2048]{2,1,0:T(8,128)}) %reduce-scatter.5.cloned.1.call-update) | async-done | bytes 5767184 | tf_op jit(solution)/shard_map/reduce_scatter | solution.py:568
  627.2 8.3 %multiply_reduce_fusion = (f32[4]{0:T(128)S(1)}, f32[4,176,2048]{2,1,0:T(8,128)}) fusion(f32[4,176,2048]{2,1,0:T(8,128)} %reduce-scatter.5.cloned.1.call-done, f32[4,176,2048]{2,1,0:T(8,128)} %param.16), kind=kLoop, calls=%fused_computation.2 | loop fusion | flops 7208956 | bytes 17301520 | tf_op jit(solution)/shard_map/reduce_sum | solution.py:511
  635.4 0.7 broadcast_in_dim.26.refs_1_
  636.1 156.3 %ortho5.1 = (bf16[4,176,2048]{2,1,0:T(8,128)(2,1)}, bf16[2,256,2048]{2,1,0:T(8,128)(2,1)}, bf16[4,1408,256]{2,1,0:T(8,128)(2,1)}) custom-call(f32[4,176,2048]{2,1,0:T(8,128)} %get-tuple-element.32.refs_0_, f32[8,128]{1,0:T(8,128)} %broadcast_in_dim.26.refs_1_, bf16[2816,2048]{1,0:T(8,128)(2,1)} %ortho1.1.refs_2_), custom_call_target="tpu_custom_call" | custom-call | flops 2000000000 | bytes 16777216 | tf_op jit(solution)/shard_map/ortho5/pallas_call | solution.py:391
  792.4 7.8 new_weights_turned.1
  800.2 7.8 fusion.4
  808.0 3.8 fusion.5
  (16 shorter events, 0.1 us)
Async XLA Ops:
  7.2 331.2 %reduce-scatter.3.cloned.1.call-start = ((), (), s32[]{:S(2)}) async-start(), calls=%async_computation.2 | async-start | bytes 37748736 | tf_op jit(solution)/shard_map/reduce_scatter | solution.py:568
  7.9 619.2 %reduce-scatter.5.cloned.1.call-start = ((), (), s32[]{:S(2)}) async-start(), calls=%async_computation.3 | async-start | bytes 51904512 | tf_op jit(solution)/shard_map/reduce_scatter | solution.py:568
  330.7 2.5 copy-start
  338.3 6.8 copy-start.1
  792.4 7.8 copy-start.3
  800.2 7.8 copy-start.2
  800.2 7.8 copy-start.4
Sparse Core Ops, SparseCore 0:
  11.5 326.8 reduce-scatter.2
  341.9 285.2 reduce-scatter.4
